TPU v7x, 32 devices: a whole 2x2x4 slice. The times are simulated.
32 devices in a mesh: head: 4 (over x, core), outer: 2 (over y), inner: 4 (over z).
Axes of the slice: x: 2, y: 2, z: 4, core: 2. Of those that a mesh axis runs over, the one named last changes fastest.
Arguments:
- queries: bfloat16 [8, 256, 4096], P(('outer', 'inner'), 'head'), may hold values from -120 to 120
- keys: bfloat16 [8, 256, 1024], P(('outer', 'inner'), 'head'), may hold values from -6 to 6
- values: bfloat16 [8, 256, 1024], P(('outer', 'inner'), 'head'), may hold values from -6 to 6
- doc_lengths: int32 [4], replicated, may hold values from 1 to 1024, 2048 in all
Outputs:
- attended: bfloat16 [8, 256, 4096], P(('outer', 'inner'), 'head')
Inputs may be any that keep to these rules, and one draw needn't show every extreme that they name: `doc_lengths`: the documents of the packed sequence in order, summing to 2048.
All inputs are finite; a program needn't handle non-finite values.
Results may differ from a plain program's by a relative error of at most 0.0044.
Values may be sent and summed in bfloat16 or wider, within the bound.
A program may use at most 64 MiB of HBM per device.

v0:
```python
import math

import jax
import jax.numpy as jnp
from jax import lax
from jax.sharding import PartitionSpec as P

HD = 128
MAXDOC = 4096


NEG_FILL = -1e30


def passed_along(block, axis, distance):
    devices = range(lax.axis_size(axis))
    route = [(i - distance, i) for i in devices if i - distance in devices]
    return lax.ppermute(block, axis, route)


def doc_index(positions, doc_lengths):
    ends = jnp.cumsum(doc_lengths)
    return jnp.sum((positions[:, None] >= ends[None, :]).astype(jnp.int32), axis=1)


def fold_block(state, key_block, value_block, offset, context):
    q_heads, q_pos, q_doc, rank, doc_lengths = context
    rows = key_block.shape[0]
    heads = key_block.shape[1] // HD
    k_pos = (rank - offset) * rows + jnp.arange(rows, dtype=jnp.int32)
    k_doc = doc_index(k_pos, doc_lengths)
    visible = (
        (k_pos[None, :] >= 0)
        & (k_pos[None, :] <= q_pos[:, None])
        & (k_doc[None, :] == q_doc[:, None])
    )
    k_heads = key_block.reshape(rows, heads, HD)
    v_heads = value_block.reshape(rows, heads, HD)
    scores = jnp.einsum("qgeh,kgh->geqk", q_heads, k_heads, preferred_element_type=jnp.float32) * (
        1.0 / math.sqrt(HD)
    )
    running, total, summed = state
    masked = jnp.where(visible[None, None], scores, NEG_FILL)
    peak = jnp.maximum(running, jnp.max(masked, axis=-1))
    factor = jnp.exp(running - peak)
    weights = jnp.where(visible[None, None], jnp.exp(scores - peak[..., None]), 0.0)
    total = total * factor + jnp.sum(weights, axis=-1)
    rounded = weights.astype(jnp.bfloat16)
    added = jnp.einsum("geqk,kgh->qgeh", rounded, v_heads, preferred_element_type=jnp.float32)
    summed = summed * jnp.transpose(factor, (2, 0, 1))[..., None] + added
    return (peak, total, summed)


def body(queries, keys, values, doc_lengths):
    q_local, k_local, v_local = (
        lax.all_to_all(queries, "head", split_axis=2, concat_axis=1, tiled=True),
        lax.all_to_all(keys, "head", split_axis=2, concat_axis=1, tiled=True),
        lax.all_to_all(values, "head", split_axis=2, concat_axis=1, tiled=True),
    )
    rows = q_local.shape[1]
    kv_heads = k_local.shape[2] // HD
    group = q_local.shape[2] // k_local.shape[2]
    q_heads = q_local[0].reshape(rows, kv_heads, group, HD)
    rank = lax.axis_index(("outer", "inner"))
    reach = min(MAXDOC // rows, lax.axis_size(("outer", "inner")) // 2)
    q_pos = rank * rows + jnp.arange(rows, dtype=jnp.int32)
    q_doc = doc_index(q_pos, doc_lengths)
    context = (q_heads, q_pos, q_doc, rank, doc_lengths)
    state = (
        jnp.full((kv_heads, group, rows), NEG_FILL, jnp.float32),
        jnp.zeros((kv_heads, group, rows), jnp.float32),
        jnp.zeros((rows, kv_heads, group, HD), jnp.float32),
    )

    def attend(state, key_block, value_block, offset):
        return fold_block(state, key_block, value_block, offset, context)

    state = attend(state, k_local[0], v_local[0], 0)
    key_window = k_local
    value_window = v_local
    held = 1
    while held < reach + 1:
        extra = min(held, reach + 1 - held)
        sent_keys, sent_values = passed_along(
            (key_window[held - extra :], value_window[held - extra :]), ("outer", "inner"), held
        )
        key_window = jnp.concatenate([sent_keys, key_window], axis=0)
        value_window = jnp.concatenate([sent_values, value_window], axis=0)
        held = held + extra

    def sweep(offset, carried):
        index = reach - offset
        key_block = lax.dynamic_index_in_dim(key_window, index, 0, keepdims=False)
        value_block = lax.dynamic_index_in_dim(value_window, index, 0, keepdims=False)
        return attend(carried, key_block, value_block, offset)

    state = lax.fori_loop(1, reach + 1, sweep, state)
    running, total, summed = state
    result = summed / jnp.transpose(total, (2, 0, 1))[..., None]
    attended = result.astype(jnp.bfloat16).reshape(1, rows, kv_heads * group * HD)
    return lax.all_to_all(attended, "head", split_axis=1, concat_axis=2, tiled=True)


def solution(mesh):
    placed = (
        P(("outer", "inner"), "head", None),
        P(("outer", "inner"), "head", None),
        P(("outer", "inner"), "head", None),
        P(),
    )
    return jax.shard_map(
        body,
        mesh=mesh,
        in_specs=placed,
        out_specs=P(("outer", "inner"), "head", None),
        check_vma=False,
    )
```

profile of v0, /device:TPU:4, one launch (start us, length us, event | category | flops | bytes accessed | tf_op | source)
XLA Modules:
  0.0 129.2 jit_solution(5051317125559907742)
XLA Ops:
  0.0 1.3 copy.102
  1.8 2.2 %reduce.1 = bf16[1024,64]{1,0:T(8,128)(2,1)S(1)} reduce(bf16[1024,1,64]{2,1,0:T(2,128)(2,1)S(1)} %bitcast.132, bf16[]{:T(256)} %broadcast.232), dimensions={1}, to_apply=%bitcast.73.reduce_sub_computation | reduce | bytes 262146
  4.9 3.3 %all-to-all-start = ((bf16[4,2,8192]{2,1,0:T(2,128)(2,1)}), bf16[4,2,8192]{2,1,0:T(2,128)(2,1)S(1)}, u32[]{:S(2)}, u32[]{:S(2)}) async-start(bf16[4,2,8192]{2,1,0:T(2,128)(2,1)} %reshape.228), calls=%async_computation | async-start | bytes 262144 | tf_op jit(solution)/shard_map/all_to_all | solution.py:57
  8.3 2.8 %copy.105 = bf16[1,64,4096]{1,0,2:T(2,128)(2,1)S(1)} copy(bf16[1,64,4096]{2,1,0:T(8,128)(2,1)S(1)} %copy-done) | data formatting | bytes 1048576 | tf_op args[0]
  11.1 22.4 %reduce = bf16[4096,64]{1,0:T(8,128)(2,1)S(1)} reduce(bf16[4096,1,64]{2,1,0:T(2,128)(2,1)S(1)} %bitcast.124, bf16[]{:T(256)} %broadcast.232), dimensions={1}, to_apply=%bitcast.75.reduce_sub_computation | reduce | bytes 1048578
  33.5 1.6 %reshape.230 = bf16[4,2,32768]{2,1,0:T(2,128)(2,1)} reshape(bf16[4096,64]{1,0:T(8,128)(2,1)S(1)} %reduce) | data formatting | bytes 1048576
  35.5 2.2 %reduce.2 = bf16[1024,64]{1,0:T(8,128)(2,1)S(1)} reduce(bf16[1024,1,64]{2,1,0:T(2,128)(2,1)S(1)} %bitcast.133, bf16[]{:T(256)} %broadcast.232), dimensions={1}, to_apply=%bitcast.77.reduce_sub_computation | reduce | bytes 262146
  38.9 3.3 %all-to-all-start.2 = ((bf16[4,2,8192]{2,1,0:T(2,128)(2,1)}), bf16[4,2,8192]{2,1,0:T(2,128)(2,1)S(1)}, u32[]{:S(2)}, u32[]{:S(2)}) async-start(bf16[4,2,8192]{2,1,0:T(2,128)(2,1)} %reshape.232), calls=%async_computation.2 | async-start | bytes 262144 | tf_op jit(solution)/shard_map/all_to_all | solution.py:58
  43.0 3.8 %all-to-all-done.2 = bf16[4,2,8192]{2,1,0:T(2,128)(2,1)S(1)} async-done(((bf16[4,2,8192]{2,1,0:T(2,128)(2,1)}), bf16[4,2,8192]{2,1,0:T(2,128)(2,1)S(1)}, u32[]{:S(2)}, u32[]{:S(2)}) %all-to-all-start.2) | async-done | bytes 131104 | tf_op jit(solution)/shard_map/all_to_all | solution.py:58
  46.8 3.5 %all-to-all-start.1 = ((bf16[4,2,32768]{2,1,0:T(2,128)(2,1)}), bf16[4,2,32768]{2,1,0:T(2,128)(2,1)S(1)}, u32[]{:S(2)}, u32[]{:S(2)}) async-start(bf16[4,2,32768]{2,1,0:T(2,128)(2,1)} %reshape.230), calls=%async_computation.1 | async-start | bytes 1048576 | tf_op jit(solution)/shard_map/all_to_all | solution.py:56
  51.0 3.5 %collective-permute-start.1 = (bf16[1,256,256]{2,1,0:T(8,128)(2,1)S(1)}, bf16[1,256,256]{2,1,0:T(8,128)(2,1)S(1)}, u32[]{:S(2)}, u32[]{:S(2)}) collective-permute-start(bf16[1,256,256]{2,1,0:T(8,128)(2,1)S(1)} %bitcast.135), channel_id=1, source_target_pairs={{0,1},{1,2},{2,3},{3,4},{4,5},{5,6},{6,7},{8,9},{9,10},{10,11},{11... | collective-permute-start | bytes 393224 | tf_op jit(solution)/shard_map/ppermute | solution.py:18
  54.5 3.5 %collective-permute-start.4 = (bf16[1,256,256]{2,1,0:T(8,128)(2,1)S(1)}, bf16[1,256,256]{2,1,0:T(8,128)(2,1)S(1)}, u32[]{:S(2)}, u32[]{:S(2)}) collective-permute-start(bf16[1,256,256]{2,1,0:T(8,128)(2,1)S(1)} %bitcast.139), channel_id=1, source_target_pairs={{0,1},{1,2},{2,3},{3,4},{4,5},{5,6},{6,7},{8,9},{9,10},{10,11},{11... | collective-permute-start | bytes 393224 | tf_op jit(solution)/shard_map/ppermute | solution.py:18
  58.9 1.3 collective-permute-start
  60.2 1.3 %collective-permute-start.3 = (bf16[1,256,256]{2,1,0:T(8,128)(2,1)S(1)}, bf16[1,256,256]{2,1,0:T(8,128)(2,1)S(1)}, u32[]{:S(2)}, u32[]{:S(2)}) collective-permute-start(bf16[1,256,256]{2,1,0:T(8,128)(2,1)S(1)} %bitcast.140), channel_id=1, source_target_pairs={{0,4},{1,5},{2,6},{3,7},{8,12},{9,13},{10,14},{11,15},{16,20},{17,... | collective-permute-start | bytes 393224 | tf_op jit(solution)/shard_map/ppermute | solution.py:18
  62.2 3.1 %collective-permute-start.2 = (bf16[2,256,256]{2,1,0:T(8,128)(2,1)}, bf16[2,256,256]{2,1,0:T(8,128)(2,1)}, u32[]{:S(2)}, u32[]{:S(2)}) collective-permute-start(bf16[2,256,256]{2,1,0:T(8,128)(2,1)} %pad_maximum_fusion.2), channel_id=1, source_target_pairs={{0,2},{1,3},{2,4},{3,5},{4,6},{5,7},{8,10},{9,11},{10,12},{11,13},... | collective-permute-start | bytes 786440 | tf_op jit(solution)/shard_map/ppermute | solution.py:18
  66.1 1.9 %collective-permute-start.5 = (bf16[2,256,256]{2,1,0:T(8,128)(2,1)}, bf16[2,256,256]{2,1,0:T(8,128)(2,1)}, u32[]{:S(2)}, u32[]{:S(2)}) collective-permute-start(bf16[2,256,256]{2,1,0:T(8,128)(2,1)} %pad_maximum_fusion.3), channel_id=1, source_target_pairs={{0,2},{1,3},{2,4},{3,5},{4,6},{5,7},{8,10},{9,11},{10,12},{11,13},... | collective-permute-start | bytes 786440 | tf_op jit(solution)/shard_map/ppermute | solution.py:18
  68.9 2.3 %copy.106 = bf16[1,64,4096]{2,1,0:T(8,128)(2,1)S(1)} copy(bf16[1,64,4096]{1,0,2:T(2,128)(2,1)S(1)} %bitcast.123) | data formatting | bytes 1048576 | tf_op jit(solution)/shard_map/all_to_all | solution.py:56
  75.2 11.6 %collective-permute-done.2 = bf16[2,256,256]{2,1,0:T(8,128)(2,1)} collective-permute-done((bf16[2,256,256]{2,1,0:T(8,128)(2,1)}, bf16[2,256,256]{2,1,0:T(8,128)(2,1)}, u32[]{:S(2)}, u32[]{:S(2)}) %collective-permute-start.2) | collective-permute-done | bytes 262176 | tf_op jit(solution)/shard_map/ppermute | solution.py:18
  86.8 1.9 %pad_maximum_fusion = bf16[5,256,256]{2,1,0:T(8,128)(2,1)} fusion(bf16[1,256,256]{2,1,0:T(8,128)(2,1)S(1)} %bitcast.138, bf16[1,256,256]{2,1,0:T(8,128)(2,1)S(1)} %collective-permute-done.1, bf16[2,256,256]{2,1,0:T(8,128)(2,1)} %collective-permute-done.2, bf16[1,256,256]{2,1,0:T(8,128)(2,1)} %collective-permute-done), kind=kLoop, calls=%fused_computation.40 | loop fusion | flops 983040 | bytes 1310720 | tf_op jit(solution)/shard_map/concatenate | solution.py:87
  88.7 2.9 %collective-permute-done.5 = bf16[2,256,256]{2,1,0:T(8,128)(2,1)} collective-permute-done((bf16[2,256,256]{2,1,0:T(8,128)(2,1)}, bf16[2,256,256]{2,1,0:T(8,128)(2,1)}, u32[]{:S(2)}, u32[]{:S(2)}) %collective-permute-start.5) | collective-permute-done | bytes 262176 | tf_op jit(solution)/shard_map/ppermute | solution.py:18
  91.6 1.9 %pad_maximum_fusion.1 = bf16[5,256,256]{2,1,0:T(8,128)(2,1)} fusion(bf16[1,256,256]{2,1,0:T(8,128)(2,1)S(1)} %bitcast.142, bf16[1,256,256]{2,1,0:T(8,128)(2,1)S(1)} %collective-permute-done.4, bf16[2,256,256]{2,1,0:T(8,128)(2,1)} %collective-permute-done.5, bf16[1,256,256]{2,1,0:T(8,128)(2,1)S(1)} %collective-permute-done.3), kind=kLoop, calls=%fused_computation.41 | loop fusion | flops 983040 | bytes 1310720 | tf_op jit(solution)/shard_map/concatenate | solution.py:88
  93.5 17.5 %while.20 = (s32[]{:T(128)}, f32[2,4,256]{2,1,0:T(4,128)S(1)}, f32[2,4,256]{2,1,0:T(4,128)S(1)}, f32[256,2,4,128]{0,3,2,1:T(8,128)S(1)}, s32[]{:T(128)}, /*index...) while((s32[]{:T(128)}, f32[2,4,256]{2,1,0:T(4,128)S(1)}, ...), condition=%wide.region_8.9_spmd.clone, body=%wide.region_4.0_spmd.clone.sunk | while | flops 274999040 | bytes 10625787 | solution.py:97
  93.8 1.0 constant_dynamic-slice_fusion.3
  94.9 1.6 %fusion.50 = (f32[2,4,256]{2,1,0:T(4,128)S(1)}, f32[2,256,256,4]{2,1,3,0:T(8,128)S(1)}) fusion(pred[256,256]{0,1:T(8,128)(4,1)S(1)} %compare_and_fusion.3, bf16[256,2,128,1]{0,2,3,1:T(8,128)(2,1)S(1)} %bitcast.121, bf16[256,2,4,128]{3,0,2,1:T(8,128)(2,1)} %get-tuple-element.533), kind=kOutput, calls=%fused_computation.3.clone.1 | convolution fusion | flops 135788544 | bytes 2826240 | tf_op jit(solution)/shard_map/while/body/eval_jaxpr/qgeh,kgh->geqk/dot_general | solution.py:39
  98.1 1.0 constant_dynamic-slice_fusion.3
  99.2 1.6 %fusion.50 = (f32[2,4,256]{2,1,0:T(4,128)S(1)}, f32[2,256,256,4]{2,1,3,0:T(8,128)S(1)}) fusion(pred[256,256]{0,1:T(8,128)(4,1)S(1)} %compare_and_fusion.3, bf16[256,2,128,1]{0,2,3,1:T(8,128)(2,1)S(1)} %bitcast.121, bf16[256,2,4,128]{3,0,2,1:T(8,128)(2,1)} %get-tuple-element.533), kind=kOutput, calls=%fused_computation.3.clone.1 | convolution fusion | flops 135788544 | bytes 2826240 | tf_op jit(solution)/shard_map/while/body/eval_jaxpr/qgeh,kgh->geqk/dot_general | solution.py:39
  102.5 1.0 constant_dynamic-slice_fusion.3
  103.6 1.6 %fusion.50 = (f32[2,4,256]{2,1,0:T(4,128)S(1)}, f32[2,256,256,4]{2,1,3,0:T(8,128)S(1)}) fusion(pred[256,256]{0,1:T(8,128)(4,1)S(1)} %compare_and_fusion.3, bf16[256,2,128,1]{0,2,3,1:T(8,128)(2,1)S(1)} %bitcast.121, bf16[256,2,4,128]{3,0,2,1:T(8,128)(2,1)} %get-tuple-element.533), kind=kOutput, calls=%fused_computation.3.clone.1 | convolution fusion | flops 135788544 | bytes 2826240 | tf_op jit(solution)/shard_map/while/body/eval_jaxpr/qgeh,kgh->geqk/dot_general | solution.py:39
  108.0 1.6 %fusion.50 = (f32[2,4,256]{2,1,0:T(4,128)S(1)}, f32[2,256,256,4]{2,1,3,0:T(8,128)S(1)}) fusion(pred[256,256]{0,1:T(8,128)(4,1)S(1)} %compare_and_fusion.3, bf16[256,2,128,1]{0,2,3,1:T(8,128)(2,1)S(1)} %bitcast.121, bf16[256,2,4,128]{3,0,2,1:T(8,128)(2,1)} %get-tuple-element.533), kind=kOutput, calls=%fused_computation.3.clone.1 | convolution fusion | flops 135788544 | bytes 2826240 | tf_op jit(solution)/shard_map/while/body/eval_jaxpr/qgeh,kgh->geqk/dot_general | solution.py:39
  111.1 1.0 copy.121
  112.1 3.7 %reduce.3 = bf16[256,1024]{1,0:T(8,128)(2,1)S(1)} reduce(bf16[256,1,1024]{2,1,0:T(2,128)(2,1)S(1)} %bitcast.127, bf16[]{:T(256)} %broadcast.232), dimensions={1}, to_apply=%bitcast.79.reduce_sub_computation | reduce | bytes 1048578
  116.1 11.5 %all_to_all.69 = bf16[4,2,32768]{2,1,0:T(2,128)(2,1)S(1)} all-to-all(bf16[4,2,32768]{2,1,0:T(2,128)(2,1)S(1)} %reshape.234), channel_id=1, replica_groups=mesh['head'=4,'outer'=2,'inner'=4] {'head'}, dimensions={0} | all-to-all | bytes 1048576 | tf_op jit(solution)/shard_map/all_to_all | solution.py:101
  (96 shorter events, 21.5 us)
Async XLA Ops:
  0.0 8.3 %copy-start = (bf16[1,64,4096]{2,1,0:T(8,128)(2,1)S(1)}, bf16[1,64,4096]{2,1,0:T(8,128)(2,1)}, u32[]{:S(2)}) copy-start(bf16[1,64,4096]{2,1,0:T(8,128)(2,1)} %param.6) | copy-start | bytes 1572868
  4.9 33.9 %all-to-all-start = ((bf16[4,2,8192]{2,1,0:T(2,128)(2,1)}), bf16[4,2,8192]{2,1,0:T(2,128)(2,1)S(1)}, u32[]{:S(2)}, u32[]{:S(2)}) async-start(bf16[4,2,8192]{2,1,0:T(2,128)(2,1)} %reshape.228), calls=%async_computation | async-start | bytes 262144 | tf_op jit(solution)/shard_map/all_to_all | solution.py:57
  11.1 24.0 %copy-start.1 = (bf16[1,64,1024]{2,1,0:T(8,128)(2,1)S(1)}, bf16[1,64,1024]{2,1,0:T(8,128)(2,1)}, u32[]{:S(2)}) copy-start(bf16[1,64,1024]{2,1,0:T(8,128)(2,1)} %param.8) | copy-start | bytes 393220
  33.5 5.1 %copy-start.3 = (s32[4]{0:T(128)S(1)}, s32[4]{0:T(128)}, u32[]{:S(2)}) copy-start(s32[4]{0:T(128)} %param.9) | copy-start | bytes 52
  38.9 7.9 %all-to-all-start.2 = ((bf16[4,2,8192]{2,1,0:T(2,128)(2,1)}), bf16[4,2,8192]{2,1,0:T(2,128)(2,1)S(1)}, u32[]{:S(2)}, u32[]{:S(2)}) async-start(bf16[4,2,8192]{2,1,0:T(2,128)(2,1)} %reshape.232), calls=%async_computation.2 | async-start | bytes 262144 | tf_op jit(solution)/shard_map/all_to_all | solution.py:58
  46.8 21.2 %all-to-all-start.1 = ((bf16[4,2,32768]{2,1,0:T(2,128)(2,1)}), bf16[4,2,32768]{2,1,0:T(2,128)(2,1)S(1)}, u32[]{:S(2)}, u32[]{:S(2)}) async-start(bf16[4,2,32768]{2,1,0:T(2,128)(2,1)} %reshape.230), calls=%async_computation.1 | async-start | bytes 1048576 | tf_op jit(solution)/shard_map/all_to_all | solution.py:56
  51.0 10.5 %collective-permute-start.1 = (bf16[1,256,256]{2,1,0:T(8,128)(2,1)S(1)}, bf16[1,256,256]{2,1,0:T(8,128)(2,1)S(1)}, u32[]{:S(2)}, u32[]{:S(2)}) collective-permute-start(bf16[1,256,256]{2,1,0:T(8,128)(2,1)S(1)} %bitcast.135), channel_id=1, source_target_pairs={{0,1},{1,2},{2,3},{3,4},{4,5},{5,6},{6,7},{8,9},{9,10},{10,11},{11... | collective-permute-start | bytes 393224 | tf_op jit(solution)/shard_map/ppermute | solution.py:18
  54.5 10.8 %collective-permute-start.4 = (bf16[1,256,256]{2,1,0:T(8,128)(2,1)S(1)}, bf16[1,256,256]{2,1,0:T(8,128)(2,1)S(1)}, u32[]{:S(2)}, u32[]{:S(2)}) collective-permute-start(bf16[1,256,256]{2,1,0:T(8,128)(2,1)S(1)} %bitcast.139), channel_id=1, source_target_pairs={{0,1},{1,2},{2,3},{3,4},{4,5},{5,6},{6,7},{8,9},{9,10},{10,11},{11... | collective-permute-start | bytes 393224 | tf_op jit(solution)/shard_map/ppermute | solution.py:18
  58.9 16.3 %collective-permute-start = (bf16[1,256,256]{2,1,0:T(8,128)(2,1)S(1)}, bf16[1,256,256]{2,1,0:T(8,128)(2,1)}, u32[]{:S(2)}, u32[]{:S(2)}) collective-permute-start(bf16[1,256,256]{2,1,0:T(8,128)(2,1)S(1)} %bitcast.136), channel_id=1, source_target_pairs={{0,4},{1,5},{2,6},{3,7},{8,12},{9,13},{10,14},{11,15},{16,20},{17,... | collective-permute-start | bytes 393224 | tf_op jit(solution)/shard_map/ppermute | solution.py:18
  60.2 28.5 %collective-permute-start.3 = (bf16[1,256,256]{2,1,0:T(8,128)(2,1)S(1)}, bf16[1,256,256]{2,1,0:T(8,128)(2,1)S(1)}, u32[]{:S(2)}, u32[]{:S(2)}) collective-permute-start(bf16[1,256,256]{2,1,0:T(8,128)(2,1)S(1)} %bitcast.140), channel_id=1, source_target_pairs={{0,4},{1,5},{2,6},{3,7},{8,12},{9,13},{10,14},{11,15},{16,20},{17,... | collective-permute-start | bytes 393224 | tf_op jit(solution)/shard_map/ppermute | solution.py:18
  62.2 24.6 %collective-permute-start.2 = (bf16[2,256,256]{2,1,0:T(8,128)(2,1)}, bf16[2,256,256]{2,1,0:T(8,128)(2,1)}, u32[]{:S(2)}, u32[]{:S(2)}) collective-permute-start(bf16[2,256,256]{2,1,0:T(8,128)(2,1)} %pad_maximum_fusion.2), channel_id=1, source_target_pairs={{0,2},{1,3},{2,4},{3,5},{4,6},{5,7},{8,10},{9,11},{10,12},{11,13},... | collective-permute-start | bytes 786440 | tf_op jit(solution)/shard_map/ppermute | solution.py:18
  66.1 25.5 %collective-permute-start.5 = (bf16[2,256,256]{2,1,0:T(8,128)(2,1)}, bf16[2,256,256]{2,1,0:T(8,128)(2,1)}, u32[]{:S(2)}, u32[]{:S(2)}) collective-permute-start(bf16[2,256,256]{2,1,0:T(8,128)(2,1)} %pad_maximum_fusion.3), channel_id=1, source_target_pairs={{0,2},{1,3},{2,4},{3,5},{4,6},{5,7},{8,10},{9,11},{10,12},{11,13},... | collective-permute-start | bytes 786440 | tf_op jit(solution)/shard_map/ppermute | solution.py:18
  72.1 1.0 copy-start.2
where the time goes:
time: 130 us; the launch traced here: 129 us
  other arithmetic  39.8 us (31%)
  starting transfers between devices  24.7 us (19%)
  local copies, waits for them, and re-layouts  23.5 us (18%)
  waiting for transfers between devices  18.3 us (14%)
  blocking collectives  11.5 us (9%)
  matrix products  10.7 us (8%)
    unnamed x4, other arithmetic  30.5 us
    ppermute x6, starting transfers between devices, passed_along(): return lax.ppermute(block, axis, route)  14.6 us
    ppermute x6, waiting for transfers between devices, passed_along(): return lax.ppermute(block, axis, route)  14.5 us
    all_to_all x1, blocking collectives, body(): lax.all_to_all(attended, 'head', split_axis=1, concat_axis=2, tiled=True)  11.5 us
    unnamed x22, local copies, waits for them, and re-layouts  11.3 us
    dot_general x5, matrix products, fold_block(): jnp.einsum('qgeh,kgh->geqk', q_heads, k_heads, preferred_element_type=jnp...  6.84 us
    dynamic_slice x8, local copies, waits for them, and re-layouts, sweep(): lax.dynamic_index_in_dim(value_window, index, 0, keepdims=False)  4.36 us
    dot_general x5, matrix products, fold_block(): jnp.einsum('geqk,kgh->qgeh', rounded, v_heads, preferred_element_type=jnp...  3.91 us
  transfers between devices with their start and end apart: 9, of which 3 were waited for; matrix products, arithmetic and copies ran while one was open for 33% of the time, Pallas kernels for 0%

commit v1 on v0

v1 whole, which is shorter than its diff:
```python
import functools
import math

import jax
import jax.numpy as jnp
from jax import lax
from jax.experimental import pallas as pl
from jax.experimental.pallas import tpu as pltpu
from jax.sharding import PartitionSpec as P

HD = 128
MAXDOC = 4096
HIDDEN = -1e30
MESH = pl.DeviceIdType.MESH


def kernel(plan, docs, q_ref, k_ref, v_ref, out, kv_in, q_in, kv, q_all, done, bias, start, peak, total, summed,
           load_sem, own_sem, kv_send, kv_recv, q_send, q_recv, win_send, win_recv, out_send, out_recv, out_own):
    heads, inner, ranks, reach, part, kv_heads, group = plan
    rows = heads * part
    width = group * HD
    me = lax.axis_index("head")
    rank = lax.axis_index("outer") * inner + lax.axis_index("inner")

    def at_rank(other):
        return {"outer": lax.div(other, inner), "inner": lax.rem(other, inner)}

    def peer(step):
        return lax.rem(me + step, heads)

    def kv_columns(owner, g):
        return pl.ds(pl.multiple_of((owner * kv_heads + g) * HD, HD), HD)

    def q_columns(owner, g):
        return pl.ds(pl.multiple_of((owner * kv_heads + g) * width, HD), width)

    def part_of(owner):
        return pl.ds(pl.multiple_of(owner * part, part), part)

    loads = [
        pltpu.make_async_copy(k_ref.at[0], kv_in.at[0], load_sem.at[0]),
        pltpu.make_async_copy(v_ref.at[0], kv_in.at[1], load_sem.at[1]),
        pltpu.make_async_copy(q_ref.at[0], q_in, load_sem.at[2]),
    ]
    for copy in loads:
        copy.start()
    own = []
    for g in range(kv_heads):
        own.append([
            pltpu.make_async_copy(k_ref.at[0, :, kv_columns(me, g)], kv.at[0, g, 0, part_of(me)], own_sem.at[g, 0]),
            pltpu.make_async_copy(v_ref.at[0, :, kv_columns(me, g)], kv.at[0, g, 1, part_of(me)], own_sem.at[g, 1]),
            pltpu.make_async_copy(q_ref.at[0, :, q_columns(me, g)], q_all.at[g, part_of(me)], own_sem.at[g, 2]),
        ])
        for copy in own[g]:
            copy.start()

    barrier = pltpu.get_barrier_semaphore()
    for step in range(1, heads):
        pl.semaphore_signal(barrier, inc=1, device_id={"head": peer(step)}, device_id_type=MESH)
    for d in range(1, reach + 1):
        @pl.when(rank + d < ranks)
        def _():
            pl.semaphore_signal(barrier, inc=1, device_id=at_rank(rank + d), device_id_type=MESH)

        @pl.when(rank >= d)
        def _():
            pl.semaphore_signal(barrier, inc=1, device_id=at_rank(rank - d), device_id_type=MESH)
    partners = heads - 1 + jnp.minimum(rank, reach) + jnp.minimum(ranks - 1 - rank, reach)
    pl.semaphore_wait(barrier, partners)

    def kv_copy(step, g, c):
        return pltpu.make_async_remote_copy(
            src_ref=kv_in.at[c, :, kv_columns(peer(step), g)],
            dst_ref=kv.at[0, g, c, part_of(me)],
            send_sem=kv_send.at[step, g, c],
            recv_sem=kv_recv.at[step, g, c],
            device_id={"head": peer(step)},
            device_id_type=MESH,
        )

    def q_copy(step, g):
        return pltpu.make_async_remote_copy(
            src_ref=q_in.at[:, q_columns(peer(step), g)],
            dst_ref=q_all.at[g, part_of(me)],
            send_sem=q_send.at[step, g],
            recv_sem=q_recv.at[step, g],
            device_id={"head": peer(step)},
            device_id_type=MESH,
        )

    def window_copy(d, g):
        return pltpu.make_async_remote_copy(
            src_ref=kv.at[0, g],
            dst_ref=kv.at[d, g],
            send_sem=win_send.at[d, g],
            recv_sem=win_recv.at[d, g],
            device_id=at_rank(lax.rem(rank + d, ranks)),
            device_id_type=MESH,
        )

    def out_copy(step, g):
        return pltpu.make_async_remote_copy(
            src_ref=done.at[g, part_of(peer(step))],
            dst_ref=out.at[0, :, q_columns(me, g)],
            send_sem=out_send.at[step, g],
            recv_sem=out_recv.at[step, g],
            device_id={"head": peer(step)},
            device_id_type=MESH,
        )

    loads[0].wait()
    loads[1].wait()
    for g in range(kv_heads):
        for step in range(1, heads):
            for c in range(2):
                kv_copy(step, g, c).start()
    loads[2].wait()
    for g in range(kv_heads):
        for step in range(1, heads):
            q_copy(step, g).start()

    pos = rank * rows + lax.broadcasted_iota(jnp.int32, (rows, rows), 0)
    first = jnp.zeros((rows, rows), jnp.int32)
    end = jnp.int32(0)
    for i in range(docs.shape[0]):
        end = end + docs[i]
        first = jnp.where(pos >= end, end, first)
    start[...] = first

    for g in range(kv_heads):
        own[g][0].wait()
        own[g][1].wait()
        for step in range(1, heads):
            for c in range(2):
                kv_copy(step, g, c).wait_recv()
        for d in range(reach, 0, -1):
            @pl.when(rank + d < ranks)
            def _():
                window_copy(d, g).start()

    power = math.log2(math.e) / math.sqrt(HD)

    def attend(g, d, opening):
        base = (rank - d) * rows
        spot = base + lax.broadcasted_iota(jnp.int32, (rows, rows), 1)
        visible = spot >= start[...]
        if opening:
            visible = visible & (spot <= rank * rows + lax.broadcasted_iota(jnp.int32, (rows, rows), 0))
        bias[...] = jnp.where(visible, 0.0, HIDDEN)
        keys = kv[d, g, 0]
        values = kv[d, g, 1]
        for e in range(group):
            query = q_all[g, :, e * HD:(e + 1) * HD]
            scores = lax.dot_general(query, keys, (((1,), (1,)), ((), ())), preferred_element_type=jnp.float32)
            scores = scores + bias[...]
            high = jnp.max(scores, axis=1, keepdims=True)
            if not opening:
                before = peak[e]
                high = jnp.maximum(high, before)
                factor = jnp.exp2((before - high) * power)
            weights = jnp.exp2((scores - high) * power)
            sums = jnp.sum(weights, axis=1, keepdims=True)
            added = jnp.dot(weights.astype(jnp.bfloat16), values, preferred_element_type=jnp.float32)
            peak[e] = high
            if opening:
                total[e] = sums
                summed[e] = added
            else:
                total[e] = total[e] * factor + sums
                summed[e] = summed[e] * factor + added

    for g in range(kv_heads):
        own[g][2].wait()
        for step in range(1, heads):
            q_copy(step, g).wait_recv()
        attend(g, 0, True)

        @pl.loop(1, reach + 1)
        def _(d):
            @pl.when(rank >= d)
            def _():
                window_copy(d, g).wait_recv()
                attend(g, d, False)

        for e in range(group):
            done[g, :, e * HD:(e + 1) * HD] = (summed[e] / total[e]).astype(jnp.bfloat16)
        for step in range(1, heads):
            out_copy(step, g).start()
        pltpu.make_async_copy(done.at[g, part_of(me)], out.at[0, :, q_columns(me, g)], out_own.at[g]).start()

    for g in range(kv_heads):
        for step in range(1, heads):
            for c in range(2):
                kv_copy(step, g, c).wait_send()
            q_copy(step, g).wait_send()
            out_copy(step, g).wait()
        pltpu.make_async_copy(done.at[g, part_of(me)], out.at[0, :, q_columns(me, g)], out_own.at[g]).wait()
        for d in range(1, reach + 1):
            @pl.when(rank + d < ranks)
            def _():
                window_copy(d, g).wait_send()


def solution(mesh):
    heads = mesh.shape["head"]
    inner = mesh.shape["inner"]
    ranks = mesh.shape["outer"] * inner

    def body(queries, keys, values, doc_lengths):
        part = queries.shape[1]
        rows = part * heads
        kv_heads = keys.shape[2] // HD // heads
        group = queries.shape[2] // keys.shape[2]
        reach = min(MAXDOC // rows, ranks // 2)
        plan = (heads, inner, ranks, reach, part, kv_heads, group)
        anywhere = pl.BlockSpec(memory_space=pl.ANY)
        dma = pltpu.SemaphoreType.DMA
        return pl.pallas_call(
            functools.partial(kernel, plan),
            out_shape=jax.ShapeDtypeStruct(queries.shape, jnp.bfloat16),
            in_specs=[pl.BlockSpec(memory_space=pltpu.SMEM), anywhere, anywhere, anywhere],
            out_specs=anywhere,
            scratch_shapes=[
                pltpu.VMEM((2, part, keys.shape[2]), jnp.bfloat16),
                pltpu.VMEM((part, queries.shape[2]), jnp.bfloat16),
                pltpu.VMEM((reach + 1, kv_heads, 2, rows, HD), jnp.bfloat16),
                pltpu.VMEM((kv_heads, rows, group * HD), jnp.bfloat16),
                pltpu.VMEM((kv_heads, rows, group * HD), jnp.bfloat16),
                pltpu.VMEM((rows, rows), jnp.float32),
                pltpu.VMEM((rows, rows), jnp.int32),
                pltpu.VMEM((group, rows, 1), jnp.float32),
                pltpu.VMEM((group, rows, 1), jnp.float32),
                pltpu.VMEM((group, rows, HD), jnp.float32),
                dma((3,)),
                dma((kv_heads, 3)),
                dma((heads, kv_heads, 2)),
                dma((heads, kv_heads, 2)),
                dma((heads, kv_heads)),
                dma((heads, kv_heads)),
                dma((reach + 1, kv_heads)),
                dma((reach + 1, kv_heads)),
                dma((heads, kv_heads)),
                dma((heads, kv_heads)),
                dma((kv_heads,)),
            ],
            compiler_params=pltpu.CompilerParams(
                collective_id=0, has_side_effects=True, vmem_limit_bytes=32 * 1024 * 1024
            ),
            name="attention",
        )(doc_lengths, queries, keys, values)

    split = P(("outer", "inner"), "head", None)
    return jax.shard_map(
        body, mesh=mesh, in_specs=(split, split, split, P()), out_specs=split, check_vma=False
    )
```

time: 130 us -> 56.2 us (0.43)
  the two profiles are of different devices: /device:TPU:4 before, /device:TPU:21 now
where the time goes in v1:
time: 56.2 us; the launch traced here: 56 us
  Pallas kernels  51.6 us (92%)
  local copies, waits for them, and re-layouts  4.3 us (8%)
    pallas_call x1, Pallas kernels, body(): pl.pallas_call(functools.partial(kernel, plan), out_shape=jax.ShapeDtypeS...  51.6 us
    unnamed x9, local copies, waits for them, and re-layouts  4.3 us

profile of v1, /device:TPU:21, one launch (start us, length us, event | category | flops | bytes accessed | tf_op | source)
XLA Modules:
  0.0 56.0 jit_solution(6884545671093532805)
XLA Ops:
  0.0 0.0 copy-start
  0.0 1.0 %copy-done = bf16[1,64,4096]{2,1,0:T(8,128)(2,1)S(1)} copy-done((bf16[1,64,4096]{2,1,0:T(8,128)(2,1)S(1)}, bf16[1,64,4096]{2,1,0:T(8,128)(2,1)}, u32[]{:S(2)}) %copy-start) | copy-done | bytes 524312
  1.0 0.0 copy-start.1
  1.0 0.9 %copy-done.1 = bf16[1,64,1024]{2,1,0:T(8,128)(2,1)S(1)} copy-done((bf16[1,64,1024]{2,1,0:T(8,128)(2,1)S(1)}, bf16[1,64,1024]{2,1,0:T(8,128)(2,1)}, u32[]{:S(2)}) %copy-start.1) | copy-done | bytes 131096
  1.9 0.0 copy-start.2
  1.9 0.9 %copy-done.2 = bf16[1,64,1024]{2,1,0:T(8,128)(2,1)S(1)} copy-done((bf16[1,64,1024]{2,1,0:T(8,128)(2,1)S(1)}, bf16[1,64,1024]{2,1,0:T(8,128)(2,1)}, u32[]{:S(2)}) %copy-start.2) | copy-done | bytes 131096
  2.9 0.0 copy-start.3
  2.9 0.7 %copy-done.3 = s32[4]{0:T(128)S(1)} copy-done((s32[4]{0:T(128)S(1)}, s32[4]{0:T(128)}, u32[]{:S(2)}) %copy-start.3) | copy-done | bytes 40
  3.5 51.6 %attention.1 = bf16[1,64,4096]{2,1,0:T(8,128)(2,1)S(1)} custom-call(s32[4]{0:T(128)S(1)} %copy-done.3, bf16[1,64,4096]{2,1,0:T(8,128)(2,1)S(1)} %copy-done, bf16[1,64,1024]{2,1,0:T(8,128)(2,1)S(1)} %copy-done.1, bf16[1,64,1024]{2,1,0:T(8,128)(2,1)S(1)} %copy-done.2), custom_call_target="tpu_custom_call" | custom-call | tf_op jit(solution)/shard_map/attention/pallas_call | solution.py:218
  55.2 0.8 %copy.6 = bf16[1,64,4096]{2,1,0:T(8,128)(2,1)} copy(bf16[1,64,4096]{2,1,0:T(8,128)(2,1)S(1)} %attention.1) | data formatting | bytes 1048576
Async XLA Ops:
  0.0 1.0 %copy-start = (bf16[1,64,4096]{2,1,0:T(8,128)(2,1)S(1)}, bf16[1,64,4096]{2,1,0:T(8,128)(2,1)}, u32[]{:S(2)}) copy-start(bf16[1,64,4096]{2,1,0:T(8,128)(2,1)} %q_ref.1) | copy-start | bytes 1572868
  1.0 0.9 %copy-start.1 = (bf16[1,64,1024]{2,1,0:T(8,128)(2,1)S(1)}, bf16[1,64,1024]{2,1,0:T(8,128)(2,1)}, u32[]{:S(2)}) copy-start(bf16[1,64,1024]{2,1,0:T(8,128)(2,1)} %k_ref.1) | copy-start | bytes 393220
  1.9 0.9 %copy-start.2 = (bf16[1,64,1024]{2,1,0:T(8,128)(2,1)S(1)}, bf16[1,64,1024]{2,1,0:T(8,128)(2,1)}, u32[]{:S(2)}) copy-start(bf16[1,64,1024]{2,1,0:T(8,128)(2,1)} %v_ref.1) | copy-start | bytes 393220
  2.9 0.7 %copy-start.3 = (s32[4]{0:T(128)S(1)}, s32[4]{0:T(128)}, u32[]{:S(2)}) copy-start(s32[4]{0:T(128)} %docs.1) | copy-start | bytes 52

commit v2 on v1

v2 whole, which is shorter than its diff:
```python
import functools
import math

import jax
import jax.numpy as jnp
from jax import lax
from jax.experimental import pallas as pl
from jax.experimental.pallas import tpu as pltpu
from jax.sharding import PartitionSpec as P

HD = 128
MAXDOC = 4096
HIDDEN = -1e30
MESH = pl.DeviceIdType.MESH


def kernel(plan, docs, q_ref, k_ref, v_ref, out, kv_in, q_in, kv, q_all, done, bias, start, peak, total, summed,
           load_sem, own_sem, kv_send, kv_recv, q_send, q_recv, up_send, down_send, direct_send, win_recv, out_send, out_recv, out_own):
    heads, inner, ranks, reach, part, kv_heads, group = plan
    rows = heads * part
    width = group * HD
    me = lax.axis_index("head")
    rank = lax.axis_index("outer") * inner + lax.axis_index("inner")

    def at_rank(other):
        return {"outer": lax.div(other, inner), "inner": lax.rem(other, inner)}

    pack = heads // 2
    half, spot_in = lax.div(me, pack), lax.rem(me, pack)

    def peer(step):
        side = half if step < pack else 1 - half
        return side * pack + lax.rem(spot_in + step % pack, pack)

    def kv_columns(owner, g):
        return pl.ds(pl.multiple_of((owner * kv_heads + g) * HD, HD), HD)

    def q_columns(owner, g):
        return pl.ds(pl.multiple_of((owner * kv_heads + g) * width, HD), width)

    def in_half(owner):
        return pl.ds(pl.multiple_of(lax.rem(owner, pack) * part, part), part)

    def part_of(owner):
        return pl.ds(pl.multiple_of(owner * part, part), part)

    place = lax.axis_index("inner")
    direct = [d for d in (reach, reach - 1) if d >= 1]
    has_up, has_down = place < inner - 1, place > 0

    def straight(d, at):
        return at < (d if d == reach else 1)

    sends = [(rank + d < ranks) & straight(d, lax.rem(rank + d, inner)) for d in direct]
    links = [(has_up, rank + 1), (has_down, rank - 1)]
    for d, wanted in zip(direct, sends):
        links.append((wanted, rank + d))
        links.append(((rank >= d) & straight(d, place), rank - d))

    loads = [
        pltpu.make_async_copy(k_ref.at[0], kv_in.at[0], load_sem.at[0]),
        pltpu.make_async_copy(v_ref.at[0], kv_in.at[1], load_sem.at[1]),
        pltpu.make_async_copy(q_ref.at[0], q_in, load_sem.at[2]),
    ]
    for copy in loads:
        copy.start()
    own = []
    for g in range(kv_heads):
        own.append([
            pltpu.make_async_copy(k_ref.at[0, :, kv_columns(me, g)], kv.at[0, g, half, 0, in_half(me)], own_sem.at[g, 0]),
            pltpu.make_async_copy(v_ref.at[0, :, kv_columns(me, g)], kv.at[0, g, half, 1, in_half(me)], own_sem.at[g, 1]),
            pltpu.make_async_copy(q_ref.at[0, :, q_columns(me, g)], q_all.at[g, part_of(me)], own_sem.at[g, 2]),
        ])
        for copy in own[g]:
            copy.start()

    barrier = pltpu.get_barrier_semaphore()
    for step in range(1, heads):
        pl.semaphore_signal(barrier, inc=1, device_id={"head": peer(step)}, device_id_type=MESH)
    partners = heads - 1
    for wanted, other in links:
        @pl.when(wanted)
        def _():
            pl.semaphore_signal(barrier, inc=1, device_id=at_rank(other), device_id_type=MESH)

        partners = partners + wanted.astype(jnp.int32)
    pl.semaphore_wait(barrier, partners)

    def kv_copy(step, g, c):
        return pltpu.make_async_remote_copy(
            src_ref=kv_in.at[c, :, kv_columns(peer(step), g)],
            dst_ref=kv.at[0, g, half, c, in_half(me)],
            send_sem=kv_send.at[step, g, c],
            recv_sem=kv_recv.at[step, g, c],
            device_id={"head": peer(step)},
            device_id_type=MESH,
        )

    def kv_arrival(step, g, c):
        side = half if step < pack else 1 - half
        source = lax.rem(spot_in + pack - step % pack, pack)
        return pltpu.make_async_remote_copy(
            src_ref=kv_in.at[c, :, kv_columns(peer(step), g)],
            dst_ref=kv.at[0, g, side, c, in_half(source)],
            send_sem=kv_send.at[step, g, c],
            recv_sem=kv_recv.at[step, g, c],
            device_id={"head": peer(step)},
            device_id_type=MESH,
        )

    def q_copy(step, g):
        return pltpu.make_async_remote_copy(
            src_ref=q_in.at[:, q_columns(peer(step), g)],
            dst_ref=q_all.at[g, part_of(me)],
            send_sem=q_send.at[step, g],
            recv_sem=q_recv.at[step, g],
            device_id={"head": peer(step)},
            device_id_type=MESH,
        )

    def window_copy(src, dst, g, part_half, other, sem):
        return pltpu.make_async_remote_copy(
            src_ref=kv.at[src, g, part_half],
            dst_ref=kv.at[dst, g, part_half],
            send_sem=sem,
            recv_sem=win_recv.at[dst, g, part_half],
            device_id=at_rank(other),
            device_id_type=MESH,
        )

    def up_copy(d, g, part_half):
        return window_copy(d, d + 1, g, part_half, lax.rem(rank + 1, ranks), up_send.at[d, g, part_half])

    def down_copy(d, g, part_half):
        return window_copy(d, d - 1, g, part_half, lax.rem(rank + ranks - 1, ranks), down_send.at[d, g, part_half])

    def direct_copy(i, g, part_half):
        return window_copy(0, direct[i], g, part_half, lax.rem(rank + direct[i], ranks), direct_send.at[i, g, part_half])

    def goes_up(d):
        return has_up & (place >= d) & (d < reach)

    def goes_down(d):
        return has_down & (place < d) & (rank >= d) & (d >= 2) & ((d < reach) | (place > 1))

    def out_copy(step, g):
        return pltpu.make_async_remote_copy(
            src_ref=done.at[g, part_of(peer(step))],
            dst_ref=out.at[0, :, q_columns(me, g)],
            send_sem=out_send.at[step, g],
            recv_sem=out_recv.at[step, g],
            device_id={"head": peer(step)},
            device_id_type=MESH,
        )

    loads[0].wait()
    loads[1].wait()
    for g in range(kv_heads):
        for step in range(1, heads):
            for c in range(2):
                kv_copy(step, g, c).start()
    loads[2].wait()
    for g in range(kv_heads):
        for step in range(1, heads):
            q_copy(step, g).start()

    pos = rank * rows + lax.broadcasted_iota(jnp.int32, (1, rows), 1)
    first = jnp.zeros((1, rows), jnp.int32)
    end = jnp.int32(0)
    for i in range(docs.shape[0]):
        end = end + docs[i]
        first = jnp.where(pos >= end, end, first)
    start[...] = first

    for side in range(2):
        part_half = half if side == 0 else 1 - half
        for g in range(kv_heads):
            if side == 0:
                own[g][0].wait()
                own[g][1].wait()
            for step in range(max(1, side * pack), (side + 1) * pack):
                for c in range(2):
                    kv_arrival(step, g, c).wait_recv()

            @pl.when(has_up)
            def _():
                up_copy(0, g, part_half).start()

            for i in range(len(direct)):
                @pl.when(sends[i])
                def _():
                    direct_copy(i, g, part_half).start()

    power = math.log2(math.e) / math.sqrt(HD)

    def attend(g, d, opening):
        spot = (rank - d) * rows + lax.broadcasted_iota(jnp.int32, (rows, rows), 0)
        visible = spot >= start[...]
        if opening:
            visible = visible & (spot <= rank * rows + lax.broadcasted_iota(jnp.int32, (rows, rows), 1))
        bias[...] = jnp.where(visible, 0.0, HIDDEN)
        keys = jnp.concatenate([kv[d, g, 0, 0], kv[d, g, 1, 0]], axis=0)
        values = jnp.concatenate([kv[d, g, 0, 1].T, kv[d, g, 1, 1].T], axis=1)
        for n in range(group):
            e = g * group + n
            query = q_all[g, :, n * HD:(n + 1) * HD]
            scores = lax.dot_general(keys, query, (((1,), (1,)), ((), ())), preferred_element_type=jnp.float32)
            scores = scores + bias[...]
            high = jnp.max(scores, axis=0, keepdims=True)
            if not opening:
                before = peak[e]
                high = jnp.maximum(high, before)
                factor = jnp.exp2((before - high) * power)
            weights = jnp.exp2((scores - high) * power)
            sums = jnp.sum(weights, axis=0, keepdims=True)
            added = jnp.dot(values, weights.astype(jnp.bfloat16), preferred_element_type=jnp.float32)
            peak[e] = high
            if opening:
                total[e] = sums
                summed[e] = added
            else:
                total[e] = total[e] * factor + sums
                summed[e] = summed[e] * factor + added

    for g in range(kv_heads):
        own[g][2].wait()
        for step in range(1, heads):
            q_copy(step, g).wait_recv()
        attend(g, 0, True)

    near = jnp.minimum(place, reach)
    across = reach - near

    @pl.loop(1, reach + 1)
    def _(k):
        d = jnp.where(near == 0, reach + 1 - k, jnp.where(k == 1, 1, jnp.where(k <= 1 + across, reach + 2 - k, k - across)))
        here = rank >= d
        for g in range(kv_heads):
            @pl.when(here)
            def _():
                for side in range(2):
                    part_half = half if side == 0 else 1 - half
                    up_arrival = window_copy(
                        0, d, g, part_half, lax.rem(rank + 1, ranks), up_send.at[0, g, part_half]
                    )
                    up_arrival.wait_recv()

                    @pl.when(goes_up(d))
                    def _():
                        up_copy(d, g, part_half).start()

                    @pl.when(goes_down(d))
                    def _():
                        down_copy(d, g, part_half).start()

                attend(g, d, False)

            @pl.when(k == reach)
            def _():
                for n in range(group):
                    e = g * group + n
                    done[g, :, n * HD:(n + 1) * HD] = (summed[e] / total[e]).astype(jnp.bfloat16).T
                for step in range(heads - 1, 0, -1):
                    out_copy(step, g).start()
                pltpu.make_async_copy(done.at[g, part_of(me)], out.at[0, :, q_columns(me, g)], out_own.at[g]).start()

    for g in range(kv_heads):
        for step in range(1, heads):
            for c in range(2):
                kv_copy(step, g, c).wait_send()
            q_copy(step, g).wait_send()
            out_copy(step, g).wait()
        pltpu.make_async_copy(done.at[g, part_of(me)], out.at[0, :, q_columns(me, g)], out_own.at[g]).wait()

        for side in range(2):
            for i in range(len(direct)):
                @pl.when(sends[i])
                def _():
                    direct_copy(i, g, side).wait_send()

            @pl.loop(0, reach + 1)
            def _(d):
                @pl.when(goes_up(d))
                def _():
                    up_copy(d, g, side).wait_send()

                @pl.when(goes_down(d))
                def _():
                    down_copy(d, g, side).wait_send()


def solution(mesh):
    heads = mesh.shape["head"]
    inner = mesh.shape["inner"]
    ranks = mesh.shape["outer"] * inner

    def body(queries, keys, values, doc_lengths):
        part = queries.shape[1]
        rows = part * heads
        kv_heads = keys.shape[2] // HD // heads
        group = queries.shape[2] // keys.shape[2]
        reach = min(MAXDOC // rows, ranks // 2)
        plan = (heads, inner, ranks, reach, part, kv_heads, group)
        anywhere = pl.BlockSpec(memory_space=pl.ANY)
        dma = pltpu.SemaphoreType.DMA
        return pl.pallas_call(
            functools.partial(kernel, plan),
            out_shape=jax.ShapeDtypeStruct(queries.shape, jnp.bfloat16),
            in_specs=[pl.BlockSpec(memory_space=pltpu.SMEM), anywhere, anywhere, anywhere],
            out_specs=anywhere,
            scratch_shapes=[
                pltpu.VMEM((2, part, keys.shape[2]), jnp.bfloat16),
                pltpu.VMEM((part, queries.shape[2]), jnp.bfloat16),
                pltpu.VMEM((reach + 1, kv_heads, 2, 2, rows // 2, HD), jnp.bfloat16),
                pltpu.VMEM((kv_heads, rows, group * HD), jnp.bfloat16),
                pltpu.VMEM((kv_heads, rows, group * HD), jnp.bfloat16),
                pltpu.VMEM((rows, rows), jnp.float32),
                pltpu.VMEM((1, rows), jnp.int32),
                pltpu.VMEM((kv_heads * group, 1, rows), jnp.float32),
                pltpu.VMEM((kv_heads * group, 1, rows), jnp.float32),
                pltpu.VMEM((kv_heads * group, HD, rows), jnp.float32),
                dma((3,)),
                dma((kv_heads, 3)),
                dma((heads, kv_heads, 2)),
                dma((heads, kv_heads, 2)),
                dma((heads, kv_heads)),
                dma((heads, kv_heads)),
                dma((reach + 1, kv_heads, 2)),
                dma((reach + 1, kv_heads, 2)),
                dma((2, kv_heads, 2)),
                dma((reach + 1, kv_heads, 2)),
                dma((heads, kv_heads)),
                dma((heads, kv_heads)),
                dma((kv_heads,)),
            ],
            compiler_params=pltpu.CompilerParams(
                collective_id=0, has_side_effects=True, vmem_limit_bytes=60 * 1024 * 1024
            ),
            name="attention",
        )(doc_lengths, queries, keys, values)

    split = P(("outer", "inner"), "head", None)
    return jax.shard_map(
        body, mesh=mesh, in_specs=(split, split, split, P()), out_specs=split, check_vma=False
    )
```

time: 56.2 us -> 43.5 us (0.77)
  the two profiles are of different devices: /device:TPU:21 before, /device:TPU:4 now
where the time goes in v2:
time: 43.5 us; the launch traced here: 43.4 us
  Pallas kernels  41.5 us (95%)
  local copies, waits for them, and re-layouts  1.87 us (4%)
    pallas_call x1, Pallas kernels, body(): pl.pallas_call(functools.partial(kernel, plan), out_shape=jax.ShapeDtypeS...  41.5 us
    unnamed x1, local copies, waits for them, and re-layouts  1.87 us

profile of v2, /device:TPU:4, one launch (start us, length us, event | category | flops | bytes accessed | tf_op | source)
XLA Modules:
  0.0 43.4 jit_solution(2143510195927723873)
XLA Ops:
  0.0 41.5 %attention.1 = bf16[1,64,4096]{2,1,0:T(8,128)(2,1)} custom-call(s32[4]{0:T(128)} %docs.1, bf16[1,64,4096]{2,1,0:T(8,128)(2,1)} %q_ref.1, bf16[1,64,1024]{2,1,0:T(8,128)(2,1)} %k_ref.1, bf16[1,64,1024]{2,1,0:T(8,128)(2,1)} %v_ref.1), custom_call_target="tpu_custom_call" | custom-call | tf_op jit(solution)/shard_map/attention/pallas_call | solution.py:306
  41.5 1.9 %copy.6 = bf16[1,64,4096]{2,1,0:T(8,128)(2,1)} copy(bf16[1,64,4096]{2,1,0:T(8,128)(2,1)} %attention.1) | data formatting | bytes 1048576

commit v3 on v2

--- a/solution.py
+++ b/solution.py
@@ -14,7 +14,7 @@
 MESH = pl.DeviceIdType.MESH
 
 
-def kernel(plan, docs, q_ref, k_ref, v_ref, out, kv_in, q_in, kv, q_all, done, bias, start, peak, total, summed,
+def kernel(plan, docs, q_ref, k_ref, v_ref, out, kv_in, q_in, kv, q_all, done, bias, held, start, peak, total, summed,
            load_sem, own_sem, kv_send, kv_recv, q_send, q_recv, up_send, down_send, direct_send, win_recv, out_send, out_recv, out_own):
     heads, inner, ranks, reach, part, kv_heads, group = plan
     rows = heads * part
@@ -201,17 +201,25 @@
         bias[...] = jnp.where(visible, 0.0, HIDDEN)
         keys = jnp.concatenate([kv[d, g, 0, 0], kv[d, g, 1, 0]], axis=0)
         values = jnp.concatenate([kv[d, g, 0, 1].T, kv[d, g, 1, 1].T], axis=1)
+        kept = bias[...]
+
+        def score(n):
+            query = q_all[g, :, n * HD:(n + 1) * HD]
+            return lax.dot_general(keys, query, (((1,), (1,)), ((), ())), preferred_element_type=jnp.float32) + kept
+
+        highs = []
+        for n in range(group):
+            scores = score(n)
+            held[n] = scores
+            highs.append(jnp.max(scores, axis=0, keepdims=True))
         for n in range(group):
             e = g * group + n
-            query = q_all[g, :, n * HD:(n + 1) * HD]
-            scores = lax.dot_general(keys, query, (((1,), (1,)), ((), ())), preferred_element_type=jnp.float32)
-            scores = scores + bias[...]
-            high = jnp.max(scores, axis=0, keepdims=True)
+            high = highs[n]
             if not opening:
                 before = peak[e]
                 high = jnp.maximum(high, before)
                 factor = jnp.exp2((before - high) * power)
-            weights = jnp.exp2((scores - high) * power)
+            weights = jnp.exp2((held[n] - high) * power)
             sums = jnp.sum(weights, axis=0, keepdims=True)
             added = jnp.dot(values, weights.astype(jnp.bfloat16), preferred_element_type=jnp.float32)
             peak[e] = high
@@ -222,37 +230,51 @@
                 total[e] = total[e] * factor + sums
                 summed[e] = summed[e] * factor + added
 
+    near = jnp.minimum(place, reach)
+    across = reach - near
+
+    def slot_at(k):
+        later = jnp.where(k == 1, 1, jnp.where(k <= 1 + across, reach + 2 - k, k - across))
+        return jnp.where(near == 0, reach + 1 - k, later)
+
+    def receive(k, g, wanted):
+        d = slot_at(k)
+
+        @pl.when(wanted & (rank >= d))
+        def _():
+            for side in range(2):
+                part_half = half if side == 0 else 1 - half
+                window_copy(0, d, g, part_half, lax.rem(rank + 1, ranks), up_send.at[0, g, part_half]).wait_recv()
+
+                @pl.when(goes_up(d))
+                def _():
+                    up_copy(d, g, part_half).start()
+
+                @pl.when(goes_down(d))
+                def _():
+                    down_copy(d, g, part_half).start()
+
+    last = slot_at(reach)
+    hurry = goes_up(last) | goes_down(last)
+
+    for g in range(kv_heads):
+        receive(1, g, True)
+        receive(2, g, True)
     for g in range(kv_heads):
         own[g][2].wait()
         for step in range(1, heads):
             q_copy(step, g).wait_recv()
         attend(g, 0, True)
 
-    near = jnp.minimum(place, reach)
-    across = reach - near
-
     @pl.loop(1, reach + 1)
     def _(k):
-        d = jnp.where(near == 0, reach + 1 - k, jnp.where(k == 1, 1, jnp.where(k <= 1 + across, reach + 2 - k, k - across)))
-        here = rank >= d
+        d = slot_at(k)
         for g in range(kv_heads):
-            @pl.when(here)
+            receive(k + 1, g, (k >= 2) & (k < reach) & ((k + 1 < reach) | hurry))
+            receive(k, g, (k == reach) & (k > 2) & jnp.logical_not(hurry))
+
+            @pl.when(rank >= d)
             def _():
-                for side in range(2):
-                    part_half = half if side == 0 else 1 - half
-                    up_arrival = window_copy(
-                        0, d, g, part_half, lax.rem(rank + 1, ranks), up_send.at[0, g, part_half]
-                    )
-                    up_arrival.wait_recv()
-
-                    @pl.when(goes_up(d))
-                    def _():
-                        up_copy(d, g, part_half).start()
-
-                    @pl.when(goes_down(d))
-                    def _():
-                        down_copy(d, g, part_half).start()
-
                 attend(g, d, False)
 
             @pl.when(k == reach)
@@ -315,6 +337,7 @@
                 pltpu.VMEM((kv_heads, rows, group * HD), jnp.bfloat16),
                 pltpu.VMEM((kv_heads, rows, group * HD), jnp.bfloat16),
                 pltpu.VMEM((rows, rows), jnp.float32),
+                pltpu.VMEM((group, rows, rows), jnp.float32),
                 pltpu.VMEM((1, rows), jnp.int32),
                 pltpu.VMEM((kv_heads * group, 1, rows), jnp.float32),
                 pltpu.VMEM((kv_heads * group, 1, rows), jnp.float32),

time: 43.5 us -> 37.3 us (0.86)
  Pallas kernels: 41.5 us -> 35.3 us
    pallas_call x1, Pallas kernels: 41.5 us -> 35.3 us  [body(): pl.pallas_call(functools.partial(kernel, plan), out_shape=jax.ShapeDtypeS...]
where the time goes in v3:
time: 37.3 us; the launch traced here: 37.2 us
  Pallas kernels  35.3 us (95%)
  local copies, waits for them, and re-layouts  1.87 us (5%)
    pallas_call x1, Pallas kernels, body(): pl.pallas_call(functools.partial(kernel, plan), out_shape=jax.ShapeDtypeS...  35.3 us
    unnamed x1, local copies, waits for them, and re-layouts  1.87 us

profile of v3, /device:TPU:4, one launch (start us, length us, event | category | flops | bytes accessed | tf_op | source)
XLA Modules:
  0.0 37.2 jit_solution(6470908119255989158)
XLA Ops:
  0.0 35.3 %attention.1 = bf16[1,64,4096]{2,1,0:T(8,128)(2,1)} custom-call(s32[4]{0:T(128)} %docs.1, bf16[1,64,4096]{2,1,0:T(8,128)(2,1)} %q_ref.1, bf16[1,64,1024]{2,1,0:T(8,128)(2,1)} %k_ref.1, bf16[1,64,1024]{2,1,0:T(8,128)(2,1)} %v_ref.1), custom_call_target="tpu_custom_call" | custom-call | tf_op jit(solution)/shard_map/attention/pallas_call | solution.py:328
  35.3 1.9 %copy.6 = bf16[1,64,4096]{2,1,0:T(8,128)(2,1)} copy(bf16[1,64,4096]{2,1,0:T(8,128)(2,1)} %attention.1) | data formatting | bytes 1048576
